TPU v7x, 32 devices: a whole 2x2x4 slice. The times are simulated.
32 devices in a mesh: expert: 8 (over z, x), dp: 4 (over y, core).
Axes of the slice: x: 2, y: 2, z: 4, core: 2. Of those that a mesh axis runs over, the one named last changes fastest.
Arguments:
- tokens: bfloat16 [8192, 2048], P(('expert', 'dp')), may hold values from -256 to 256
- routes: int32 [8192, 2], P(('expert', 'dp')), may hold values from 0 to 31, all different within a row
- priority: int32 [32, 256], P(('expert', 'dp')), may hold values from 0 to 255, each once within a row
- router: bfloat16 [2048, 32], replicated, may hold values from -3 to 3
- w_in: bfloat16 [32, 2048, 1024], P(('expert', 'dp')), may hold values from -0.125 to 0.125
- w_out: bfloat16 [32, 2048, 1024], P(('expert', 'dp')), may hold values from -0.1875 to 0.1875
Outputs:
- mixed: bfloat16 [8192, 2048], P(('expert', 'dp'))
- aux_loss: float32 [], replicated
Inputs may be any that keep to these rules, and one draw needn't show every extreme that they name: `routes`: a token's two experts differ; every expert is named by some token. `priority`: each group's 256 tokens hold every rank once.
All inputs are finite; a program needn't handle non-finite values.
Results may differ from a plain program's by a relative error of at most 0.0014.
The roundings to bfloat16 on the way count: a program that leaves them out, or rounds other values in their place, can miss the bound.
Values may be sent and summed in bfloat16 or wider, within the bound.
A program may use at most 64 MiB of HBM per device.

v0:
```python
import jax
import jax.numpy as jnp
from jax import lax
from jax.sharding import PartitionSpec as P


def send_rows(outgoing):
    column = lax.all_to_all(outgoing, "dp", split_axis=1, concat_axis=1, tiled=True)
    arrived = lax.all_to_all(column, "expert", split_axis=0, concat_axis=0, tiled=True)
    return arrived


def return_rows(produced):
    column = lax.all_to_all(produced, "expert", split_axis=0, concat_axis=0, tiled=True)
    returned = lax.all_to_all(column, "dp", split_axis=1, concat_axis=1, tiled=True)
    return returned


def shards(tokens, routes, priority, router, w_in, w_out):
    group_rows = tokens.shape[0]
    width = tokens.shape[1]
    experts = router.shape[1]
    slot_cap = 4 * group_rows // experts
    owner_count = lax.axis_size("expert")
    column_count = lax.axis_size("dp")
    logits = jnp.dot(tokens, router, preferred_element_type=jnp.float32)
    probs = jax.nn.softmax(logits, axis=-1)
    expert_grid = lax.broadcasted_iota(jnp.int32, (group_rows, experts), 1)
    first = routes[:, 0]
    second = routes[:, 1]
    first_hot = (expert_grid == first[:, None]).astype(jnp.float32)
    second_hot = (expert_grid == second[:, None]).astype(jnp.float32)
    logit_first = jnp.sum(logits * first_hot, axis=1)
    logit_second = jnp.sum(logits * second_hot, axis=1)
    gate_first = jax.nn.sigmoid(logit_first - logit_second).astype(jnp.bfloat16)
    gate_second = jax.nn.sigmoid(logit_second - logit_first).astype(jnp.bfloat16)
    ranks = priority[0]
    earlier = (ranks[None, :] < ranks[:, None]).astype(jnp.bfloat16)
    before_first = jnp.dot(
        earlier, first_hot.astype(jnp.bfloat16), preferred_element_type=jnp.float32
    )
    before_second = jnp.dot(
        earlier, second_hot.astype(jnp.bfloat16), preferred_element_type=jnp.float32
    )
    first_load = jnp.sum(first_hot, axis=0)
    pos_first = jnp.sum(before_first * first_hot, axis=1).astype(jnp.int32)
    pos_second = jnp.sum((before_second + first_load[None, :]) * second_hot, axis=1).astype(
        jnp.int32
    )
    slot_first = jnp.where(pos_first < slot_cap, first * slot_cap + pos_first, -1)
    slot_second = jnp.where(pos_second < slot_cap, second * slot_cap + pos_second, -1)
    slot_grid = lax.broadcasted_iota(jnp.int32, (experts * slot_cap, group_rows), 0)
    dispatch = ((slot_grid == slot_first[None, :]) | (slot_grid == slot_second[None, :])).astype(
        jnp.bfloat16
    )
    outgoing = jnp.dot(dispatch, tokens, preferred_element_type=jnp.float32).astype(jnp.bfloat16)
    outgoing = outgoing.reshape(owner_count, column_count, slot_cap, width)
    arrived = send_rows(outgoing)
    expert_rows = arrived.reshape(experts * slot_cap, width)
    hidden = jax.nn.relu(jnp.dot(expert_rows, w_in[0], preferred_element_type=jnp.float32)).astype(
        jnp.bfloat16
    )
    produced = lax.dot_general(
        hidden, w_out[0], (((1,), (1,)), ((), ())), preferred_element_type=jnp.float32
    ).astype(jnp.bfloat16)
    returned = return_rows(produced.reshape(owner_count, column_count, slot_cap, width))
    returned = returned.reshape(experts * slot_cap, width)
    token_grid = lax.broadcasted_iota(jnp.int32, (group_rows, experts * slot_cap), 1)
    nothing = jnp.zeros((), jnp.bfloat16)
    combine = jnp.where(
        token_grid == slot_first[:, None], gate_first[:, None], nothing
    ) + jnp.where(token_grid == slot_second[:, None], gate_second[:, None], nothing)
    mixed = jnp.dot(combine, returned, preferred_element_type=jnp.float32).astype(jnp.bfloat16)
    prob_sum = jnp.sum(probs, axis=0)
    statistics = jnp.stack([prob_sum, first_load], axis=0)
    all_tokens = group_rows * owner_count * column_count
    totals = lax.psum(statistics, ("expert", "dp"))
    aux_loss = experts * jnp.sum(totals[0] / all_tokens * (totals[1] / all_tokens))
    return (mixed, aux_loss)


def solution(mesh):
    placed = (
        P(("expert", "dp"), None),
        P(("expert", "dp"), None),
        P(("expert", "dp"), None),
        P(),
        P(("expert", "dp"), None, None),
        P(("expert", "dp"), None, None),
    )
    return jax.shard_map(
        shards,
        mesh=mesh,
        in_specs=placed,
        out_specs=(P(("expert", "dp"), None), P()),
        check_vma=False,
    )
```

profile of v0, /device:TPU:0, one launch (start us, length us, event | category | flops | bytes accessed | tf_op | source)
XLA Modules:
  0.0 359.2 jit_solution(15551242178874864396)
XLA Ops:
  0.6 0.0 copy-start
  0.6 0.8 fusion.38
  1.4 1.0 fusion.10
  2.5 0.0 copy-done
  2.5 1.3 fusion.39
  3.9 0.1 divide_reduce_fusion
  4.0 1.0 fusion.11
  5.0 1.3 convolution_convert_fusion
  6.3 0.6 copy.14
  6.9 52.2 %all_to_all.20 = bf16[8,4,32,2048]{3,2,0,1:T(8,128)(2,1)S(1)} all-to-all(bf16[8,4,32,2048]{3,2,0,1:T(8,128)(2,1)S(1)} %copy.14), channel_id=1, replica_groups=mesh['expert'=8,'dp'=4] {'dp'}, dimensions={1} | all-to-all | bytes 8388608 | tf_op jit(solution)/shard_map/all_to_all | solution.py:8
  59.1 0.6 copy.15
  59.7 0.0 copy-start.2
  59.7 98.9 %all_to_all.21 = bf16[8,4,32,2048]{3,2,1,0:T(8,128)(2,1)S(1)} all-to-all(bf16[8,4,32,2048]{3,2,1,0:T(8,128)(2,1)S(1)} %copy.15), channel_id=1, replica_groups=mesh['expert'=8,'dp'=4] {'expert'}, dimensions={0} | all-to-all | bytes 8388608 | tf_op jit(solution)/shard_map/all_to_all | solution.py:9
  158.6 0.0 copy-done.2
  158.6 0.0 copy-start.3
  158.6 4.7 %maximum_convert_fusion = bf16[1024,1024]{1,0:T(8,128)(2,1)S(1)} fusion(bf16[1024,2048]{1,0:T(8,128)(2,1)S(1)} %bitcast.31, bf16[1,2048,1024]{2,1,0:T(8,128)(2,1)S(1)} %copy-done.2), kind=kOutput, calls=%fused_computation.4 | convolution fusion | flops 4297064448 | bytes 10485760 | tf_op jit(solution)/shard_map/dot_general | solution.py:60
  163.3 0.0 copy-done.3
  163.3 4.8 %fusion.4 = bf16[1024,2048]{1,0:T(8,128)(2,1)S(1)} fusion(bf16[1024,1024]{1,0:T(8,128)(2,1)S(1)} %maximum_convert_fusion, bf16[1,2048,1024]{2,1,0:T(8,128)(2,1)S(1)} %copy-done.3), kind=kOutput, calls=%fused_computation.6 | convolution fusion | flops 4297064448 | bytes 10485760 | tf_op jit(solution)/shard_map/dot_general | solution.py:63
  168.1 96.2 %all_to_all.22 = bf16[8,4,32,2048]{3,2,1,0:T(8,128)(2,1)S(1)} all-to-all(bf16[8,4,32,2048]{3,2,1,0:T(8,128)(2,1)S(1)} %bitcast.32), channel_id=1, replica_groups=mesh['expert'=8,'dp'=4] {'expert'}, dimensions={0} | all-to-all | bytes 8388608 | tf_op jit(solution)/shard_map/all_to_all | solution.py:14
  264.2 2.3 copy.16
  266.5 0.0 copy-start.1
  266.5 5.0 %all-to-all-start.3 = ((bf16[8,4,32,2048]{3,2,0,1:T(8,128)(2,1)}), bf16[8,4,32,2048]{3,2,0,1:T(8,128)(2,1)}, u32[]{:S(2)}, u32[]{:S(2)}) async-start(bf16[8,4,32,2048]{3,2,0,1:T(8,128)(2,1)} %copy.16), calls=%async_computation.3 | async-start | bytes 8388608 | tf_op jit(solution)/shard_map/all_to_all | solution.py:15
  271.6 80.2 %psum.7 = f32[2,32]{1,0:T(2,128)S(1)} all-reduce(f32[2,32]{1,0:T(2,128)S(1)} %pad_maximum_fusion), channel_id=1, replica_groups=mesh['expert'=8,'dp'=4] {'expert','dp'}, use_global_device_ids=true, to_apply=%region_8.9 | all-reduce | flops 64 | bytes 512 | tf_op jit(solution)/shard_map/psum | solution.py:77
  351.8 0.6 multiply_reduce_fusion
  353.0 0.0 copy-done.1
  353.1 0.0 all-to-all-done.3
  353.1 2.5 copy.17
  355.6 2.4 convolution_convert_fusion.1
  (7 shorter events, 0.1 us)
Async XLA Ops:
  0.6 1.8 copy-start
  59.7 98.9 %copy-start.2 = (bf16[1,2048,1024]{2,1,0:T(8,128)(2,1)S(1)}, bf16[1,2048,1024]{2,1,0:T(8,128)(2,1)}, u32[]{:S(2)}) copy-start(bf16[1,2048,1024]{2,1,0:T(8,128)(2,1)} %param.10) | copy-start | bytes 12582916
  158.6 4.7 %copy-start.3 = (bf16[1,2048,1024]{2,1,0:T(8,128)(2,1)S(1)}, bf16[1,2048,1024]{2,1,0:T(8,128)(2,1)}, u32[]{:S(2)}) copy-start(bf16[1,2048,1024]{2,1,0:T(8,128)(2,1)} %param.11) | copy-start | bytes 12582916
  266.5 86.5 %copy-start.1 = (s32[256,2]{0,1:T(2,128)S(1)}, s32[256,2]{0,1:T(2,128)}, u32[]{:S(2)}) copy-start(s32[256,2]{0,1:T(2,128)} %param.7) | copy-start | bytes 6148
  266.5 86.5 %all-to-all-start.3 = ((bf16[8,4,32,2048]{3,2,0,1:T(8,128)(2,1)}), bf16[8,4,32,2048]{3,2,0,1:T(8,128)(2,1)}, u32[]{:S(2)}, u32[]{:S(2)}) async-start(bf16[8,4,32,2048]{3,2,0,1:T(8,128)(2,1)} %copy.16), calls=%async_computation.3 | async-start | bytes 8388608 | tf_op jit(solution)/shard_map/all_to_all | solution.py:15
where the time goes:
time: 360 us; the launch traced here: 359 us
  blocking collectives  327 us (91%)
  matrix products  16.6 us (5%)
  local copies, waits for them, and re-layouts  6.74 us (2%)
  starting transfers between devices  4.99 us (1%)
    all_to_all x1, blocking collectives, send_rows(): lax.all_to_all(column, 'expert', split_axis=0, concat_axis=0, tiled=True)  98.9 us
    all_to_all x1, blocking collectives, return_rows(): lax.all_to_all(produced, 'expert', split_axis=0, concat_axis=0, tiled=True)  96.2 us
    psum x1, blocking collectives, shards(): totals = lax.psum(statistics, ('expert', 'dp'))  80.2 us
    all_to_all x1, blocking collectives, send_rows(): lax.all_to_all(outgoing, 'dp', split_axis=1, concat_axis=1, tiled=True)  52.2 us
  transfers between devices with their start and end apart: 1, of which 0 were waited for; matrix products, arithmetic and copies ran while one was open for 0% of the time, Pallas kernels for 0%

commit v1 on v0

--- a/solution.py
+++ b/solution.py
@@ -74,7 +74,8 @@
     prob_sum = jnp.sum(probs, axis=0)
     statistics = jnp.stack([prob_sum, first_load], axis=0)
     all_tokens = group_rows * owner_count * column_count
-    totals = lax.psum(statistics, ("expert", "dp"))
+    inner = lax.psum(statistics, "dp")
+    totals = lax.psum(inner, "expert")
     aux_loss = experts * jnp.sum(totals[0] / all_tokens * (totals[1] / all_tokens))
     return (mixed, aux_loss)
 

time: 360 us -> 348 us (0.967)
  blocking collectives: 327 us -> 316 us
    psum x1 -> x2, blocking collectives: 80.2 us -> 68.8 us  [the longest x1 49.6 us: shards(): inner = lax.psum(statistics, 'dp')]
where the time goes in v1:
time: 348 us
  blocking collectives  316 us (91%)
  matrix products  16.6 us (5%)
  local copies, waits for them, and re-layouts  6.74 us (2%)
  starting transfers between devices  4.99 us (1%)
    all_to_all x1, blocking collectives, send_rows(): lax.all_to_all(column, 'expert', split_axis=0, concat_axis=0, tiled=True)  98.9 us
    all_to_all x1, blocking collectives, return_rows(): lax.all_to_all(produced, 'expert', split_axis=0, concat_axis=0, tiled=True)  96.2 us
    all_to_all x1, blocking collectives, send_rows(): lax.all_to_all(outgoing, 'dp', split_axis=1, concat_axis=1, tiled=True)  52.2 us
    psum x1, blocking collectives, shards(): inner = lax.psum(statistics, 'dp')  49.6 us
    psum x1, blocking collectives, shards(): totals = lax.psum(inner, 'expert')  19.2 us
  transfers between devices with their start and end apart: 1, of which 0 were waited for; matrix products, arithmetic and copies ran while one was open for 0% of the time, Pallas kernels for 0%

profile of v1, /device:TPU:0, one launch (start us, length us, event | category | flops | bytes accessed | tf_op | source)
XLA Modules:
  0.0 347.8 jit_solution(9459706262804889092)
XLA Ops:
  0.6 0.0 copy-start
  0.6 0.8 fusion.38
  1.4 1.0 fusion.10
  2.5 0.0 copy-done
  2.5 1.3 fusion.39
  3.9 0.1 divide_reduce_fusion
  4.0 1.0 fusion.11
  5.0 1.3 convolution_convert_fusion
  6.3 0.6 copy.14
  6.9 52.2 %all_to_all.20 = bf16[8,4,32,2048]{3,2,0,1:T(8,128)(2,1)S(1)} all-to-all(bf16[8,4,32,2048]{3,2,0,1:T(8,128)(2,1)S(1)} %copy.14), channel_id=1, replica_groups=mesh['expert'=8,'dp'=4] {'dp'}, dimensions={1} | all-to-all | bytes 8388608 | tf_op jit(solution)/shard_map/all_to_all | solution.py:8
  59.1 0.6 copy.15
  59.7 0.0 copy-start.2
  59.7 98.9 %all_to_all.21 = bf16[8,4,32,2048]{3,2,1,0:T(8,128)(2,1)S(1)} all-to-all(bf16[8,4,32,2048]{3,2,1,0:T(8,128)(2,1)S(1)} %copy.15), channel_id=1, replica_groups=mesh['expert'=8,'dp'=4] {'expert'}, dimensions={0} | all-to-all | bytes 8388608 | tf_op jit(solution)/shard_map/all_to_all | solution.py:9
  158.6 0.0 copy-done.2
  158.6 0.0 copy-start.3
  158.6 4.7 %maximum_convert_fusion = bf16[1024,1024]{1,0:T(8,128)(2,1)S(1)} fusion(bf16[1024,2048]{1,0:T(8,128)(2,1)S(1)} %bitcast.31, bf16[1,2048,1024]{2,1,0:T(8,128)(2,1)S(1)} %copy-done.2), kind=kOutput, calls=%fused_computation.4 | convolution fusion | flops 4297064448 | bytes 10485760 | tf_op jit(solution)/shard_map/dot_general | solution.py:60
  163.3 0.0 copy-done.3
  163.3 4.8 %fusion.4 = bf16[1024,2048]{1,0:T(8,128)(2,1)S(1)} fusion(bf16[1024,1024]{1,0:T(8,128)(2,1)S(1)} %maximum_convert_fusion, bf16[1,2048,1024]{2,1,0:T(8,128)(2,1)S(1)} %copy-done.3), kind=kOutput, calls=%fused_computation.6 | convolution fusion | flops 4297064448 | bytes 10485760 | tf_op jit(solution)/shard_map/dot_general | solution.py:63
  168.1 96.2 %all_to_all.22 = bf16[8,4,32,2048]{3,2,1,0:T(8,128)(2,1)S(1)} all-to-all(bf16[8,4,32,2048]{3,2,1,0:T(8,128)(2,1)S(1)} %bitcast.32), channel_id=1, replica_groups=mesh['expert'=8,'dp'=4] {'expert'}, dimensions={0} | all-to-all | bytes 8388608 | tf_op jit(solution)/shard_map/all_to_all | solution.py:14
  264.2 2.3 copy.16
  266.5 0.0 copy-start.1
  266.5 5.0 %all-to-all-start.3 = ((bf16[8,4,32,2048]{3,2,0,1:T(8,128)(2,1)}), bf16[8,4,32,2048]{3,2,0,1:T(8,128)(2,1)}, u32[]{:S(2)}, u32[]{:S(2)}) async-start(bf16[8,4,32,2048]{3,2,0,1:T(8,128)(2,1)} %copy.16), calls=%async_computation.3 | async-start | bytes 8388608 | tf_op jit(solution)/shard_map/all_to_all | solution.py:15
  271.6 49.6 %psum.14 = f32[2,32]{1,0:T(2,128)S(1)} all-reduce(f32[2,32]{1,0:T(2,128)S(1)} %pad_maximum_fusion), channel_id=1, replica_groups=mesh['expert'=8,'dp'=4] {'dp'}, use_global_device_ids=true, to_apply=%region_8.9 | all-reduce | flops 64 | bytes 512 | tf_op jit(solution)/shard_map/psum | solution.py:77
  321.2 19.2 %psum.15 = f32[2,32]{1,0:T(2,128)S(1)} all-reduce(f32[2,32]{1,0:T(2,128)S(1)} %psum.14), channel_id=1, replica_groups=mesh['expert'=8,'dp'=4] {'expert'}, use_global_device_ids=true, to_apply=%region_9.10 | all-reduce | flops 64 | bytes 512 | tf_op jit(solution)/shard_map/psum | solution.py:78
  340.4 0.6 multiply_reduce_fusion
  341.7 0.0 copy-done.1
  341.7 0.0 all-to-all-done.3
  341.7 2.5 copy.17
  344.2 2.4 convolution_convert_fusion.1
  (7 shorter events, 0.1 us)
Async XLA Ops:
  0.6 1.8 copy-start
  59.7 98.9 %copy-start.2 = (bf16[1,2048,1024]{2,1,0:T(8,128)(2,1)S(1)}, bf16[1,2048,1024]{2,1,0:T(8,128)(2,1)}, u32[]{:S(2)}) copy-start(bf16[1,2048,1024]{2,1,0:T(8,128)(2,1)} %param.10) | copy-start | bytes 12582916
  158.6 4.7 %copy-start.3 = (bf16[1,2048,1024]{2,1,0:T(8,128)(2,1)S(1)}, bf16[1,2048,1024]{2,1,0:T(8,128)(2,1)}, u32[]{:S(2)}) copy-start(bf16[1,2048,1024]{2,1,0:T(8,128)(2,1)} %param.11) | copy-start | bytes 12582916
  266.5 75.1 %copy-start.1 = (s32[256,2]{0,1:T(2,128)S(1)}, s32[256,2]{0,1:T(2,128)}, u32[]{:S(2)}) copy-start(s32[256,2]{0,1:T(2,128)} %param.7) | copy-start | bytes 6148
  266.5 75.2 %all-to-all-start.3 = ((bf16[8,4,32,2048]{3,2,0,1:T(8,128)(2,1)}), bf16[8,4,32,2048]{3,2,0,1:T(8,128)(2,1)}, u32[]{:S(2)}, u32[]{:S(2)}) async-start(bf16[8,4,32,2048]{3,2,0,1:T(8,128)(2,1)} %copy.16), calls=%async_computation.3 | async-start | bytes 8388608 | tf_op jit(solution)/shard_map/all_to_all | solution.py:15
